TPU v7x, 32 devices: a whole 2x2x4 slice. The times are simulated.
32 devices in a mesh: wide: 16 (over z, y, x), narrow: 2 (over core).
Axes of the slice: x: 2, y: 2, z: 4, core: 2. Of those that a mesh axis runs over, the one named last changes fastest.
Arguments:
- node_latent: bfloat16 [4096, 512], P(('wide', 'narrow')), may hold values from -6 to 6
- edge_latent: bfloat16 [16384, 512], P(('wide', 'narrow')), may hold values from -6 to 6
- node_cotangent: bfloat16 [4096, 512], P(('wide', 'narrow')), may hold values from -6 to 6
- w_first: bfloat16 [1536, 512], replicated, may hold values from -2 to 2
- bias_first: bfloat16 [512], replicated, may hold values from -4 to 4
- w_second: bfloat16 [512, 512], replicated, may hold values from -2 to 2
- bias_second: bfloat16 [512], replicated, may hold values from -4 to 4
- norm_gain: bfloat16 [512], replicated, may hold values from 0.099609375 to 1.8984375
- send_map: int32 [32, 4, 64], P(('wide', 'narrow')), may hold values from -1 to 127, as said below
- edge_sender: int32 [16384], P(('wide', 'narrow')), may hold values from 0 to 383, as said below
- edge_receiver: int32 [16384], P(('wide', 'narrow')), may hold values from 0 to 127
Outputs:
- node_grad: bfloat16 [4096, 512], P(('wide', 'narrow'))
- edge_grad: bfloat16 [16384, 512], P(('wide', 'narrow'))
- first_update: float32 [1536, 512], P('wide')
- second_update: float32 [512, 512], P('wide')
Inputs may be any that keep to these rules, and one draw needn't show every extreme that they name: `send_map`: -1 marks an unused slot; in each row the used slots come first, at most 64, about a third of them on average; in every draw some partition uses all 64 slots toward a wide neighbour; partitions at narrow index 0 send nothing toward block 3 of a lower neighbour and those at the last narrow index nothing toward a higher one. `edge_sender`: a value below 128 is a local node; 128 + k * 64 + s names slot s of received block k, and only slots that the sending partition uses are named.
All inputs are finite; a program needn't handle non-finite values.
Results may differ from a plain program's by a relative error of at most 0.0085.
Values may be sent and summed in bfloat16 or wider, within the bound.
No kernel may reach another device: no remote copies, remote signals or barrier semaphores. Data moves between devices by JAX's collectives and lax.ppermute only.
A program may use at most 64 MiB of HBM per device.

v0:
```python
import math
import jax
import jax.numpy as jnp
from jax import lax
from jax.sharding import PartitionSpec as P


def shifted(value, axis, steps):
    count = lax.axis_size(axis)
    pairs = [(source, (source + steps) % count) for source in range(count)]
    return lax.ppermute(value, axis, pairs)


def shifted_2(block, axis, distance):
    devices = range(lax.axis_size(axis))
    route = [(i - distance, i) for i in devices if i - distance in devices]
    return lax.ppermute(block, axis, route)


def neighbours(blocks, direction):
    higher = shifted(blocks[0], "wide", direction)
    lower = shifted(blocks[1], "wide", -direction)
    up_side = shifted_2(blocks[2], "narrow", direction)
    down_side = shifted_2(blocks[3], "narrow", -direction)
    return jnp.stack([higher, lower, up_side, down_side], 0)


def norm_parts(second_pre):
    mean_value = jnp.mean(second_pre, -1, keepdims=True)
    centered = second_pre - mean_value
    variance = jnp.mean(centered * centered, -1, keepdims=True)
    inv_std = lax.rsqrt(variance + 1e-05)
    return (centered * inv_std, inv_std)


def clip_share(grad_share, grad_sq, weight_sq, fan_rows):
    unit_ratio = jnp.sqrt((grad_sq + 1e-06) / (weight_sq + 1e-06))
    mean_ratio = jnp.mean(unit_ratio)
    factor = jnp.minimum(
        1.0 / (mean_ratio * jnp.sqrt(weight_sq + 1e-06)), 1.0 / jnp.sqrt(grad_sq + 1e-06)
    )
    return grad_share * factor * math.sqrt(fan_rows)


def edge_contract(hot_table, values):
    return lax.dot_general(
        hot_table,
        values,
        (((0,), (0,)), ((), ())),
        precision=lax.Precision.HIGHEST,
        preferred_element_type=jnp.float32,
    )


def per_device(
    node_latent,
    edge_latent,
    node_cotangent,
    w_first,
    bias_first,
    w_second,
    bias_second,
    norm_gain,
    send_map,
    edge_sender,
    edge_receiver,
):
    node_count, feature_width = node_latent.shape
    halo_slots = send_map.shape[2]
    table_rows = node_count + 4 * halo_slots
    send_hot = (send_map[0][:, :, None] == jnp.arange(node_count, dtype=jnp.int32)).astype(
        jnp.bfloat16
    )
    outgoing = jnp.einsum(
        "khn,nd->khd", send_hot, node_latent, preferred_element_type=jnp.float32
    ).astype(jnp.bfloat16)
    received = neighbours(outgoing, 1)
    node_table = jnp.concatenate([node_latent, received.reshape(4 * halo_slots, feature_width)], 0)
    sender_hot = (edge_sender[:, None] == jnp.arange(table_rows, dtype=jnp.int32)).astype(
        jnp.bfloat16
    )
    receiver_hot = (edge_receiver[:, None] == jnp.arange(node_count, dtype=jnp.int32)).astype(
        jnp.bfloat16
    )
    sender_rows = jnp.dot(sender_hot, node_table, preferred_element_type=jnp.float32).astype(
        jnp.bfloat16
    )
    receiver_rows = jnp.dot(receiver_hot, node_latent, preferred_element_type=jnp.float32).astype(
        jnp.bfloat16
    )
    inputs = jnp.concatenate([edge_latent, sender_rows, receiver_rows], 1)
    preact = jnp.dot(inputs, w_first, preferred_element_type=jnp.float32) + bias_first.astype(
        jnp.float32
    )
    activation = jax.nn.silu(preact).astype(jnp.bfloat16)
    second_pre = jnp.dot(
        activation, w_second, preferred_element_type=jnp.float32
    ) + bias_second.astype(jnp.float32)
    normalized, inv_std = norm_parts(second_pre)
    upstream = jnp.dot(receiver_hot, node_cotangent, preferred_element_type=jnp.float32)
    scaled = upstream * norm_gain.astype(jnp.float32)
    norm_back = (
        inv_std
        * (
            scaled
            - jnp.mean(scaled, -1, keepdims=True)
            - normalized * jnp.mean(scaled * normalized, -1, keepdims=True)
        )
    ).astype(jnp.bfloat16)
    second_grad = lax.dot_general(
        activation, norm_back, (((0,), (0,)), ((), ())), preferred_element_type=jnp.float32
    )
    sigmoid_pre = jax.nn.sigmoid(preact)
    pre_back = (
        jnp.dot(norm_back, w_second.T, preferred_element_type=jnp.float32)
        * sigmoid_pre
        * (1.0 + preact * (1.0 - sigmoid_pre))
    ).astype(jnp.bfloat16)
    first_grad = lax.dot_general(
        inputs, pre_back, (((0,), (0,)), ((), ())), preferred_element_type=jnp.float32
    )
    input_back = jnp.dot(pre_back, w_first.T, preferred_element_type=jnp.float32)
    edge_grad = (upstream + input_back[:, :feature_width]).astype(jnp.bfloat16)
    table_grad = edge_contract(
        sender_hot.astype(jnp.float32), input_back[:, feature_width : 2 * feature_width]
    )
    receiver_grad = edge_contract(
        receiver_hot.astype(jnp.float32), input_back[:, 2 * feature_width :]
    )
    halo_grad = table_grad[node_count:].reshape(4, halo_slots, feature_width).astype(jnp.bfloat16)
    returned = neighbours(halo_grad, -1)
    back = jnp.einsum("khn,khd->nd", send_hot, returned, preferred_element_type=jnp.float32)
    node_grad = (
        node_cotangent.astype(jnp.float32) + table_grad[:node_count] + receiver_grad + back
    ).astype(jnp.bfloat16)
    wide_count = lax.axis_size("wide")
    first_rows = w_first.shape[0] // wide_count
    second_rows = w_second.shape[0] // wide_count
    first_weight_sq = jnp.sum(jnp.square(w_first.astype(jnp.float32)), 0)
    second_weight_sq = jnp.sum(jnp.square(w_second.astype(jnp.float32)), 0)
    first_total, second_total = lax.psum((first_grad, second_grad), ("wide", "narrow"))
    position = lax.axis_index("wide")
    first_share = lax.dynamic_slice_in_dim(first_total, position * first_rows, first_rows, 0)
    second_share = lax.dynamic_slice_in_dim(second_total, position * second_rows, second_rows, 0)
    first_grad_sq = jnp.sum(first_total * first_total, 0)
    second_grad_sq = jnp.sum(second_total * second_total, 0)
    first_update = clip_share(first_share, first_grad_sq, first_weight_sq, w_first.shape[0])
    second_update = clip_share(second_share, second_grad_sq, second_weight_sq, w_second.shape[0])
    return (node_grad, edge_grad, first_update, second_update)


def solution(mesh):
    return jax.shard_map(
        per_device,
        mesh=mesh,
        in_specs=(
            P(("wide", "narrow"), None),
            P(("wide", "narrow"), None),
            P(("wide", "narrow"), None),
            P(),
            P(),
            P(),
            P(),
            P(),
            P(("wide", "narrow"), None, None),
            P(("wide", "narrow")),
            P(("wide", "narrow")),
        ),
        out_specs=(
            P(("wide", "narrow"), None),
            P(("wide", "narrow"), None),
            P("wide", None),
            P("wide", None),
        ),
        check_vma=False,
    )
```

profile of v0, /device:TPU:0, one launch (start us, length us, event | category | flops | bytes accessed | tf_op | source)
XLA Modules:
  0.0 192.4 jit_solution(14532633733271048976)
XLA Ops:
  7.2 0.0 copy-start.4
  7.2 0.0 copy-start.8
  7.2 0.0 copy-start.1
  7.2 0.0 all-reduce.3.cloned.1.call-start
  7.2 1.3 convolution_convert_fusion.2
  8.6 1.3 collective-permute-start.3
  9.9 3.0 %collective-permute-start.2 = (bf16[64,512]{1,0:T(8,128)(2,1)S(1)}, bf16[64,512]{1,0:T(8,128)(2,1)S(1)}, u32[]{:S(2)}, u32[]{:S(2)}) collective-permute-start(bf16[64,512]{1,0:T(8,128)(2,1)S(1)} %get-tuple-element.18), channel_id=1, source_target_pairs={{0,1},{2,3},{4,5},{6,7},{8,9},{10,11},{12,13},{14,15},{16,17},{18,... | collective-permute-start | bytes 196616 | tf_op jit(solution)/shard_map/ppermute | solution.py:17
  12.9 7.0 %collective-permute-start.1 = (bf16[64,512]{1,0:T(8,128)(2,1)S(1)}, bf16[64,512]{1,0:T(8,128)(2,1)S(1)}, u32[]{:S(2)}, u32[]{:S(2)}) collective-permute-start(bf16[64,512]{1,0:T(8,128)(2,1)S(1)} %get-tuple-element.19), channel_id=1, source_target_pairs={{0,30},{2,0},{4,2},{6,4},{8,6},{10,8},{12,10},{14,12},{16,14},{18,... | collective-permute-start | bytes 196616 | tf_op jit(solution)/shard_map/ppermute | solution.py:11
  19.9 0.0 collective-permute-start
  19.9 1.3 convolution_convert_fusion.1
  21.3 0.7 convert_element_type.56
  22.0 0.7 convert_element_type.55
  22.6 1.3 copy.15
  23.9 0.7 convert_element_type.53
  24.6 0.0 collective-permute-done.3
  24.6 0.0 collective-permute-done.2
  24.6 0.0 collective-permute-done.1
  24.6 3.2 %collective-permute-done = bf16[64,512]{1,0:T(8,128)(2,1)S(1)} collective-permute-done((bf16[64,512]{1,0:T(8,128)(2,1)S(1)}, bf16[64,512]{1,0:T(8,128)(2,1)S(1)}, u32[]{:S(2)}, u32[]{:S(2)}) %collective-permute-start) | collective-permute-done | bytes 65568 | tf_op jit(solution)/shard_map/ppermute | solution.py:11
  27.8 0.0 copy-done.4
  27.8 0.0 copy-done.8
  27.9 0.6 convolution_convert_fusion
  28.5 0.0 copy-done.1
  28.5 0.0 copy-start.5
  28.5 1.0 convolution_add_fusion.1
  29.5 0.0 copy-done.5
  29.5 0.6 fusion.33
  30.2 0.2 multiply_reduce_fusion.5
  30.4 0.1 copy-done.6
  30.4 0.0 copy-done.7
  30.4 0.5 multiply_reduce_fusion.6
  31.0 0.3 multiply_convert_fusion
  31.3 0.7 fusion.1
  31.9 0.1 copy-done
  32.0 1.5 fusion.31
  33.5 0.0 copy-done.3
  33.5 2.7 %fusion.7 = f32[1536,512]{1,0:T(8,128)} fusion(bf16[512,512]{1,0:T(8,128)(2,1)S(1)} %fusion.1, bf16[512,512]{0,1:T(8,128)(2,1)S(1)} %convolution_convert_fusion.1, bf16[512,512]{0,1:T(8,128)(2,1)S(1)} %convolution_convert_fusion, bf16[512,512]{0,1:T(8,128)(2,1)S(1)} %copy.15), kind=kOutput, calls=%fused_computation.28 | convolution fusion | flops 810024960 | bytes 5242880 | tf_op jit(solution)/shard_map/dot_general | solution.py:119
  36.2 0.0 all-reduce.3.cloned.1.call-update
  36.2 0.2 multiply_reduce_fusion.2
  36.4 0.4 multiply_reduce_fusion
  36.8 2.6 %fusion.35 = f32[512,1536]{1,0:T(8,128)S(1)} fusion(bf16[512,512]{1,0:T(8,128)(2,1)} %copy-done.3, bf16[1536,512]{1,0:T(8,128)(2,1)} %param.14), kind=kOutput, calls=%fused_computation.74 | convolution fusion | flops 805306368 | bytes 5242880 | tf_op jit(solution)/shard_map/dot_general | solution.py:122
  39.3 1.0 slice.69
  40.4 1.8 fusion.34
  42.3 1.9 collective-permute-start.7
  44.2 1.3 collective-permute-start.6
  45.5 0.1 collective-permute-start.5
  45.5 5.6 %collective-permute-start.4 = (bf16[64,512]{1,0:T(8,128)(2,1)S(1)}, bf16[64,512]{1,0:T(8,128)(2,1)}, u32[]{:S(2)}, u32[]{:S(2)}) collective-permute-start(bf16[64,512]{1,0:T(8,128)(2,1)S(1)} %get-tuple-element.12), channel_id=1, source_target_pairs={{0,30},{2,0},{4,2},{6,4},{8,6},{10,8},{12,10},{14,12},{16,14},{18,... | collective-permute-start | bytes 196616 | tf_op jit(solution)/shard_map/ppermute | solution.py:11
  51.1 2.6 %copy.18 = f32[512,512]{0,1:T(8,128)} copy(f32[512,512]{1,0:T(8,128)} %slice.69) | data formatting | bytes 2097152
  53.7 2.6 %add_convert_fusion = bf16[512,512]{0,1:T(8,128)(2,1)} fusion(f32[512,512]{0,1:T(8,128)} %copy-done, f32[512,512]{0,1:T(8,128)} %copy.18), kind=kLoop, calls=%fused_computation.20 | loop fusion | flops 524288 | bytes 2621440 | tf_op jit(solution)/shard_map/convert_element_type | solution.py:123
  56.2 2.3 %convolution_add_fusion.2 = f32[128,512]{1,0:T(8,128)} fusion(f32[512,1536]{1,0:T(8,128)S(1)} %fusion.35, f32[384,512]{1,0:T(8,128)} %get-tuple-element.24, bf16[128,512]{1,0:T(8,128)(2,1)S(1)} %copy-done.6, s32[512]{0:T(512)S(1)} %copy-done.7), kind=kOutput, calls=%fused_computation.12 | convolution fusion | flops 402915328 | bytes 1705984 | tf_op jit(solution)/shard_map/dot_general | solution.py:46
  58.5 2.0 %copy.17 = bf16[512,512]{1,0:T(8,128)(2,1)} copy(bf16[512,512]{0,1:T(8,128)(2,1)} %add_convert_fusion) | data formatting | bytes 1048576
  60.6 0.0 collective-permute-done.7
  60.6 0.0 collective-permute-done.6
  60.6 0.0 collective-permute-done.5
  60.6 0.0 collective-permute-done.4
  60.6 0.0 copy-done.9
  60.6 2.0 %fusion.3 = bf16[128,512]{1,0:T(8,128)(2,1)} fusion(f32[128,512]{1,0:T(8,128)} %convolution_add_fusion.2, bf16[1,64,512]{2,1,0:T(8,128)(2,1)} %bitcast.14, bf16[1,64,512]{2,1,0:T(8,128)(2,1)} %bitcast.13, bf16[1,64,512]{2,1,0:T(8,128)(2,1)} %bitcast.12, bf16[1,64,512]{2,1,0:T(8,128)(2,1)} %bitcast.11, s32[4,64]{1,0:T(4,128)S(1)} %bitcast.43), kind=kOutput, calls=%fused_computation.14 | convolution fusion | flops 34111488 | bytes 656384 | tf_op jit(solution)/shard_map/khn,khd->nd/dot_general | solution.py:132
  62.6 115.6 %all-reduce.3.cloned.1.call-done = (f32[1536,512]{1,0:T(8,128)}, f32[512,512]{1,0:T(8,128)}) async-done(((f32[1536,512]{1,0:T(8,128)}, f32[512,512]{1,0:T(8,128)}), (f32[1536,512]{1,0:T(8,128)}, f32[512,512]{1,0:T(8,128)})) %all-reduce.3.cloned.1.call-update) | async-done | bytes 4194320 | tf_op jit(solution)/shard_map/psum | solution.py:141
  178.3 2.3 %multiply_reduce_fusion.1 = f32[512]{0:T(512)S(1)} fusion(f32[1536,512]{1,0:T(8,128)} %get-tuple-element.10), kind=kLoop, calls=%fused_computation.1 | loop fusion | flops 1572352 | bytes 3147776 | tf_op jit(solution)/shard_map/reduce_sum | solution.py:145
  180.5 0.6 sqrt_reduce_fusion.1
  181.8 0.0 copy-done.2
  181.8 0.1 multiply_reduce_fusion.3
  182.0 0.6 sqrt_reduce_fusion
  183.2 1.6 multiply_multiply_fusion
  184.9 0.6 multiply_multiply_fusion.1
  (14 shorter events, 0.1 us)
Async XLA Ops:
  7.2 20.7 %copy-start.4 = (bf16[128,512]{1,0:T(8,128)(2,1)S(1)}, bf16[128,512]{1,0:T(8,128)(2,1)}, u32[]{:S(2)}) copy-start(bf16[128,512]{1,0:T(8,128)(2,1)} %param.11) | copy-start | bytes 393220
  7.2 20.7 %copy-start.8 = (s32[512]{0:T(512)S(1)}, s32[512]{0:T(512)}, u32[]{:S(2)}) copy-start(s32[512]{0:T(512)} %param.20) | copy-start | bytes 6148
  7.2 21.3 %copy-start.1 = (bf16[1536,512]{1,0:T(8,128)(2,1)S(1)}, bf16[1536,512]{1,0:T(8,128)(2,1)}, u32[]{:S(2)}) copy-start(bf16[1536,512]{1,0:T(8,128)(2,1)} %param.14) | copy-start | bytes 4718596
  7.2 171.1 %all-reduce.3.cloned.1.call-start = ((), (), s32[]{:S(2)}) async-start(), calls=%async_computation | async-start | bytes 8388608 | tf_op jit(solution)/shard_map/psum | solution.py:141
  8.6 16.0 %collective-permute-start.3 = (bf16[64,512]{1,0:T(8,128)(2,1)S(1)}, bf16[64,512]{1,0:T(8,128)(2,1)S(1)}, u32[]{:S(2)}, u32[]{:S(2)}) collective-permute-start(bf16[64,512]{1,0:T(8,128)(2,1)S(1)} %get-tuple-element.17), channel_id=1, source_target_pairs={{1,0},{3,2},{5,4},{7,6},{9,8},{11,10},{13,12},{15,14},{17,16},{19,... | collective-permute-start | bytes 196616 | tf_op jit(solution)/shard_map/ppermute | solution.py:17
  9.9 14.7 %collective-permute-start.2 = (bf16[64,512]{1,0:T(8,128)(2,1)S(1)}, bf16[64,512]{1,0:T(8,128)(2,1)S(1)}, u32[]{:S(2)}, u32[]{:S(2)}) collective-permute-start(bf16[64,512]{1,0:T(8,128)(2,1)S(1)} %get-tuple-element.18), channel_id=1, source_target_pairs={{0,1},{2,3},{4,5},{6,7},{8,9},{10,11},{12,13},{14,15},{16,17},{18,... | collective-permute-start | bytes 196616 | tf_op jit(solution)/shard_map/ppermute | solution.py:17
  12.9 11.7 %collective-permute-start.1 = (bf16[64,512]{1,0:T(8,128)(2,1)S(1)}, bf16[64,512]{1,0:T(8,128)(2,1)S(1)}, u32[]{:S(2)}, u32[]{:S(2)}) collective-permute-start(bf16[64,512]{1,0:T(8,128)(2,1)S(1)} %get-tuple-element.19), channel_id=1, source_target_pairs={{0,30},{2,0},{4,2},{6,4},{8,6},{10,8},{12,10},{14,12},{16,14},{18,... | collective-permute-start | bytes 196616 | tf_op jit(solution)/shard_map/ppermute | solution.py:11
  19.9 7.9 %collective-permute-start = (bf16[64,512]{1,0:T(8,128)(2,1)S(1)}, bf16[64,512]{1,0:T(8,128)(2,1)S(1)}, u32[]{:S(2)}, u32[]{:S(2)}) collective-permute-start(bf16[64,512]{1,0:T(8,128)(2,1)S(1)} %get-tuple-element.16), channel_id=1, source_target_pairs={{0,2},{2,4},{4,6},{6,8},{8,10},{10,12},{12,14},{14,16},{16,18},{18... | collective-permute-start | bytes 196616 | tf_op jit(solution)/shard_map/ppermute | solution.py:11
  28.5 1.0 copy-start.5
  29.5 0.9 copy-start.6
  29.5 0.9 copy-start.7
  30.9 1.1 copy-start
  32.0 1.5 copy-start.3
  42.3 18.3 %collective-permute-start.7 = (bf16[64,512]{1,0:T(8,128)(2,1)S(1)}, bf16[64,512]{1,0:T(8,128)(2,1)}, u32[]{:S(2)}, u32[]{:S(2)}) collective-permute-start(bf16[64,512]{1,0:T(8,128)(2,1)S(1)} %get-tuple-element.13), channel_id=1, source_target_pairs={{0,1},{2,3},{4,5},{6,7},{8,9},{10,11},{12,13},{14,15},{16,17},{18,... | collective-permute-start | bytes 196616 | tf_op jit(solution)/shard_map/ppermute | solution.py:17
  44.2 16.4 %collective-permute-start.6 = (bf16[64,512]{1,0:T(8,128)(2,1)S(1)}, bf16[64,512]{1,0:T(8,128)(2,1)}, u32[]{:S(2)}, u32[]{:S(2)}) collective-permute-start(bf16[64,512]{1,0:T(8,128)(2,1)S(1)} %get-tuple-element.14), channel_id=1, source_target_pairs={{1,0},{3,2},{5,4},{7,6},{9,8},{11,10},{13,12},{15,14},{17,16},{19,... | collective-permute-start | bytes 196616 | tf_op jit(solution)/shard_map/ppermute | solution.py:17
  45.5 15.1 %collective-permute-start.5 = (bf16[64,512]{1,0:T(8,128)(2,1)S(1)}, bf16[64,512]{1,0:T(8,128)(2,1)}, u32[]{:S(2)}, u32[]{:S(2)}) collective-permute-start(bf16[64,512]{1,0:T(8,128)(2,1)S(1)} %get-tuple-element.15), channel_id=1, source_target_pairs={{0,2},{2,4},{4,6},{6,8},{8,10},{10,12},{12,14},{14,16},{16,18},{18... | collective-permute-start | bytes 196616 | tf_op jit(solution)/shard_map/ppermute | solution.py:11
  45.5 15.0 %collective-permute-start.4 = (bf16[64,512]{1,0:T(8,128)(2,1)S(1)}, bf16[64,512]{1,0:T(8,128)(2,1)}, u32[]{:S(2)}, u32[]{:S(2)}) collective-permute-start(bf16[64,512]{1,0:T(8,128)(2,1)S(1)} %get-tuple-element.12), channel_id=1, source_target_pairs={{0,30},{2,0},{4,2},{6,4},{8,6},{10,8},{12,10},{14,12},{16,14},{18,... | collective-permute-start | bytes 196616 | tf_op jit(solution)/shard_map/ppermute | solution.py:11
  53.7 6.9 %copy-start.9 = (s32[1,4,64]{2,1,0:T(4,128)S(1)}, s32[1,4,64]{2,1,0:T(4,128)}, u32[]{:S(2)}) copy-start(s32[1,4,64]{2,1,0:T(4,128)} %param.19) | copy-start | bytes 3076
  178.3 3.5 %copy-start.2 = (f32[512,512]{1,0:T(8,128)S(1)}, f32[512,512]{1,0:T(8,128)}, u32[]{:S(2)}) copy-start(f32[512,512]{1,0:T(8,128)} %get-tuple-element.11) | copy-start | bytes 3145732
Sparse Core Ops, SparseCore 0:
  36.3 141.9 all-reduce.2
where the time goes:
time: 193 us; the launch traced here: 192 us
  waiting for transfers between devices  119 us (62%)
  starting transfers between devices  20.2 us (10%)
  matrix products  18.9 us (10%)
  between operations  15.6 us (8%)
  other arithmetic  11.6 us (6%)
  local copies, waits for them, and re-layouts  7.15 us (4%)
    psum x1, waiting for transfers between devices, per_device(): lax.psum((first_grad, second_grad), ('wide', 'narrow'))  116 us
    ppermute x4, starting transfers between devices, shifted(): return lax.ppermute(value, axis, pairs)  12.7 us
    ppermute x4, starting transfers between devices, shifted_2(): return lax.ppermute(block, axis, route)  7.52 us
    unnamed x23, local copies, waits for them, and re-layouts  6.07 us
    dot_general x2, matrix products, edge_contract(): lax.dot_general(hot_table, values, (((0,), (0,)), ((), ())), precision=la...  4.11 us
  transfers between devices with their start and end apart: 9, of which 2 were waited for; matrix products, arithmetic and copies ran while one was open for 12% of the time, Pallas kernels for 0%

commit v1 on v0

--- a/solution.py
+++ b/solution.py
@@ -3,6 +3,10 @@
 import jax.numpy as jnp
 from jax import lax
 from jax.sharding import PartitionSpec as P
+
+
+def _point_lines(xx, across, bus_axis):
+    return lax.psum(lax.psum(xx, axis_name=across), axis_name=bus_axis)
 
 
 def shifted(value, axis, steps):
@@ -138,7 +142,7 @@
     second_rows = w_second.shape[0] // wide_count
     first_weight_sq = jnp.sum(jnp.square(w_first.astype(jnp.float32)), 0)
     second_weight_sq = jnp.sum(jnp.square(w_second.astype(jnp.float32)), 0)
-    first_total, second_total = lax.psum((first_grad, second_grad), ("wide", "narrow"))
+    first_total, second_total = _point_lines((first_grad, second_grad), "wide", bus_axis="narrow")
     position = lax.axis_index("wide")
     first_share = lax.dynamic_slice_in_dim(first_total, position * first_rows, first_rows, 0)
     second_share = lax.dynamic_slice_in_dim(second_total, position * second_rows, second_rows, 0)

time: 193 us -> 247 us (1.28)
  waiting for transfers between devices: 119 us -> 173 us
    psum x1 -> x2, waiting for transfers between devices: 116 us -> 170 us  [_point_lines(): return lax.psum(lax.psum(xx, axis_name=across), axis_name=bus_axis)]
  transfers between devices with their start and end apart: 9 -> 10, of which waited for: 2 -> 3; matrix products, arithmetic and copies ran while one was open for 12% -> 9% of each run, Pallas kernels for 0% -> 0%
where the time goes in v1:
time: 247 us
  waiting for transfers between devices  173 us (70%)
  starting transfers between devices  20.4 us (8%)
  matrix products  19 us (8%)
  between operations  15.6 us (6%)
  other arithmetic  11.5 us (5%)
  local copies, waits for them, and re-layouts  7.17 us (3%)
    psum x2, waiting for transfers between devices, _point_lines(): return lax.psum(lax.psum(xx, axis_name=across), axis_name=bus_axis)  170 us
    ppermute x4, starting transfers between devices, shifted(): return lax.ppermute(value, axis, pairs)  12.7 us
    ppermute x4, starting transfers between devices, shifted_2(): return lax.ppermute(block, axis, route)  7.63 us
    unnamed x23, local copies, waits for them, and re-layouts  6.09 us
  transfers between devices with their start and end apart: 10, of which 3 were waited for; matrix products, arithmetic and copies ran while one was open for 9% of the time, Pallas kernels for 0%

profile of v1, /device:TPU:0, one launch (start us, length us, event | category | flops | bytes accessed | tf_op | source)
XLA Modules:
  0.0 246.8 jit_solution(4955441316672108275)
XLA Ops:
  7.2 0.0 copy-start.4
  7.2 0.0 copy-start.8
  7.2 0.0 copy-start.1
  7.2 0.0 all-reduce.5.cloned.1.call-start
  7.2 1.3 convolution_convert_fusion.2
  8.6 1.3 collective-permute-start.3
  9.9 3.0 %collective-permute-start.2 = (bf16[64,512]{1,0:T(8,128)(2,1)S(1)}, bf16[64,512]{1,0:T(8,128)(2,1)S(1)}, u32[]{:S(2)}, u32[]{:S(2)}) collective-permute-start(bf16[64,512]{1,0:T(8,128)(2,1)S(1)} %get-tuple-element.20), channel_id=1, source_target_pairs={{0,1},{2,3},{4,5},{6,7},{8,9},{10,11},{12,13},{14,15},{16,17},{18,... | collective-permute-start | bytes 196616 | tf_op jit(solution)/shard_map/ppermute | solution.py:21
  12.9 7.0 %collective-permute-start.1 = (bf16[64,512]{1,0:T(8,128)(2,1)S(1)}, bf16[64,512]{1,0:T(8,128)(2,1)S(1)}, u32[]{:S(2)}, u32[]{:S(2)}) collective-permute-start(bf16[64,512]{1,0:T(8,128)(2,1)S(1)} %get-tuple-element.21), channel_id=1, source_target_pairs={{0,30},{2,0},{4,2},{6,4},{8,6},{10,8},{12,10},{14,12},{16,14},{18,... | collective-permute-start | bytes 196616 | tf_op jit(solution)/shard_map/ppermute | solution.py:15
  19.9 0.0 collective-permute-start
  19.9 1.3 convolution_convert_fusion.1
  21.3 0.7 convert_element_type.56
  22.0 0.7 convert_element_type.55
  22.6 1.3 copy.15
  23.9 0.7 convert_element_type.53
  24.6 0.0 collective-permute-done.3
  24.6 0.0 collective-permute-done.2
  24.6 0.0 collective-permute-done.1
  24.6 3.2 %collective-permute-done = bf16[64,512]{1,0:T(8,128)(2,1)S(1)} collective-permute-done((bf16[64,512]{1,0:T(8,128)(2,1)S(1)}, bf16[64,512]{1,0:T(8,128)(2,1)S(1)}, u32[]{:S(2)}, u32[]{:S(2)}) %collective-permute-start) | collective-permute-done | bytes 65568 | tf_op jit(solution)/shard_map/ppermute | solution.py:15
  27.8 0.0 copy-done.4
  27.8 0.0 copy-done.8
  27.9 0.6 convolution_convert_fusion
  28.5 0.0 copy-done.1
  28.5 0.0 copy-start.5
  28.5 1.0 convolution_add_fusion.1
  29.5 0.0 copy-done.5
  29.5 0.6 fusion.33
  30.2 0.2 multiply_reduce_fusion.5
  30.4 0.1 copy-done.6
  30.4 0.5 multiply_reduce_fusion.6
  31.0 0.3 multiply_convert_fusion
  31.3 0.7 fusion.1
  31.9 0.1 copy-done
  32.0 1.5 fusion.31
  33.5 2.7 %fusion.7 = f32[1536,512]{1,0:T(8,128)} fusion(bf16[512,512]{1,0:T(8,128)(2,1)S(1)} %fusion.1, bf16[512,512]{0,1:T(8,128)(2,1)S(1)} %convolution_convert_fusion.1, bf16[512,512]{0,1:T(8,128)(2,1)S(1)} %convolution_convert_fusion, bf16[512,512]{0,1:T(8,128)(2,1)S(1)} %copy.15), kind=kOutput, calls=%fused_computation.28 | convolution fusion | flops 810024960 | bytes 5242880 | tf_op jit(solution)/shard_map/dot_general | solution.py:123
  36.2 0.0 all-reduce.5.cloned.1.call-update
  36.2 0.0 all-reduce.7.cloned.1.call-start
  36.2 166.6 %all-reduce.5.cloned.1.call-done = (f32[1536,512]{1,0:T(8,128)}, f32[512,512]{1,0:T(8,128)}) async-done(((f32[1536,512]{1,0:T(8,128)}, f32[512,512]{1,0:T(8,128)}), (f32[1536,512]{1,0:T(8,128)}, f32[512,512]{1,0:T(8,128)})) %all-reduce.5.cloned.1.call-update) | async-done | bytes 4194320 | tf_op jit(solution)/shard_map/psum | solution.py:9
  202.9 0.0 all-reduce.7.cloned.1.call-update
  202.9 0.2 multiply_reduce_fusion.2
  203.1 0.4 multiply_reduce_fusion
  203.5 2.6 %fusion.35 = f32[512,1536]{1,0:T(8,128)S(1)} fusion(bf16[512,512]{1,0:T(8,128)(2,1)} %copy-done.3, bf16[1536,512]{1,0:T(8,128)(2,1)} %param.14), kind=kOutput, calls=%fused_computation.74 | convolution fusion | flops 805306368 | bytes 5242880 | tf_op jit(solution)/shard_map/dot_general | solution.py:126
  206.1 1.0 slice.69
  207.1 1.8 fusion.34
  209.0 2.0 collective-permute-start.7
  211.0 1.3 collective-permute-start.6
  212.3 1.5 collective-permute-start.5
  213.8 4.2 %collective-permute-start.4 = (bf16[64,512]{1,0:T(8,128)(2,1)S(1)}, bf16[64,512]{1,0:T(8,128)(2,1)}, u32[]{:S(2)}, u32[]{:S(2)}) collective-permute-start(bf16[64,512]{1,0:T(8,128)(2,1)S(1)} %get-tuple-element.14), channel_id=1, source_target_pairs={{0,30},{2,0},{4,2},{6,4},{8,6},{10,8},{12,10},{14,12},{16,14},{18,... | collective-permute-start | bytes 196616 | tf_op jit(solution)/shard_map/ppermute | solution.py:15
  218.0 2.5 %copy.18 = f32[512,512]{0,1:T(8,128)} copy(f32[512,512]{1,0:T(8,128)} %slice.69) | data formatting | bytes 2097152
  220.5 2.5 %add_convert_fusion = bf16[512,512]{0,1:T(8,128)(2,1)} fusion(f32[512,512]{0,1:T(8,128)} %copy-done, f32[512,512]{0,1:T(8,128)} %copy.18), kind=kLoop, calls=%fused_computation.20 | loop fusion | flops 524288 | bytes 2621440 | tf_op jit(solution)/shard_map/convert_element_type | solution.py:127
  223.0 2.3 convolution_add_fusion.2
  225.3 2.1 copy.17
  227.4 0.0 collective-permute-done.7
  227.4 0.0 collective-permute-done.6
  227.4 0.0 collective-permute-done.5
  227.4 0.0 collective-permute-done.4
  227.4 2.1 fusion.3
  229.5 3.3 %all-reduce.7.cloned.1.call-done = (f32[1536,512]{1,0:T(8,128)}, f32[512,512]{1,0:T(8,128)}) async-done(((f32[1536,512]{1,0:T(8,128)}, f32[512,512]{1,0:T(8,128)}), (f32[1536,512]{1,0:T(8,128)}, f32[512,512]{1,0:T(8,128)})) %all-reduce.7.cloned.1.call-update) | async-done | bytes 4194320 | tf_op jit(solution)/shard_map/psum | solution.py:9
  232.8 2.3 multiply_reduce_fusion.1
  235.0 0.6 sqrt_reduce_fusion.1
  236.3 0.0 copy-done.2
  236.3 0.1 multiply_reduce_fusion.3
  236.4 0.6 sqrt_reduce_fusion
  237.7 1.6 multiply_multiply_fusion
  239.4 0.6 multiply_multiply_fusion.1
  (17 shorter events, 0.1 us)
Async XLA Ops:
  7.2 20.7 %copy-start.4 = (bf16[128,512]{1,0:T(8,128)(2,1)S(1)}, bf16[128,512]{1,0:T(8,128)(2,1)}, u32[]{:S(2)}) copy-start(bf16[128,512]{1,0:T(8,128)(2,1)} %param.11) | copy-start | bytes 393220
  7.2 20.7 %copy-start.8 = (s32[512]{0:T(512)S(1)}, s32[512]{0:T(512)}, u32[]{:S(2)}) copy-start(s32[512]{0:T(512)} %param.20) | copy-start | bytes 6148
  7.2 21.3 %copy-start.1 = (bf16[1536,512]{1,0:T(8,128)(2,1)S(1)}, bf16[1536,512]{1,0:T(8,128)(2,1)}, u32[]{:S(2)}) copy-start(bf16[1536,512]{1,0:T(8,128)(2,1)} %param.14) | copy-start | bytes 4718596
  7.2 195.7 %all-reduce.5.cloned.1.call-start = ((), (), s32[]{:S(2)}) async-start(), calls=%async_computation | async-start | bytes 8388608 | tf_op jit(solution)/shard_map/psum | solution.py:9
  8.6 16.0 %collective-permute-start.3 = (bf16[64,512]{1,0:T(8,128)(2,1)S(1)}, bf16[64,512]{1,0:T(8,128)(2,1)S(1)}, u32[]{:S(2)}, u32[]{:S(2)}) collective-permute-start(bf16[64,512]{1,0:T(8,128)(2,1)S(1)} %get-tuple-element.19), channel_id=1, source_target_pairs={{1,0},{3,2},{5,4},{7,6},{9,8},{11,10},{13,12},{15,14},{17,16},{19,... | collective-permute-start | bytes 196616 | tf_op jit(solution)/shard_map/ppermute | solution.py:21
  9.9 14.7 %collective-permute-start.2 = (bf16[64,512]{1,0:T(8,128)(2,1)S(1)}, bf16[64,512]{1,0:T(8,128)(2,1)S(1)}, u32[]{:S(2)}, u32[]{:S(2)}) collective-permute-start(bf16[64,512]{1,0:T(8,128)(2,1)S(1)} %get-tuple-element.20), channel_id=1, source_target_pairs={{0,1},{2,3},{4,5},{6,7},{8,9},{10,11},{12,13},{14,15},{16,17},{18,... | collective-permute-start | bytes 196616 | tf_op jit(solution)/shard_map/ppermute | solution.py:21
  12.9 11.7 %collective-permute-start.1 = (bf16[64,512]{1,0:T(8,128)(2,1)S(1)}, bf16[64,512]{1,0:T(8,128)(2,1)S(1)}, u32[]{:S(2)}, u32[]{:S(2)}) collective-permute-start(bf16[64,512]{1,0:T(8,128)(2,1)S(1)} %get-tuple-element.21), channel_id=1, source_target_pairs={{0,30},{2,0},{4,2},{6,4},{8,6},{10,8},{12,10},{14,12},{16,14},{18,... | collective-permute-start | bytes 196616 | tf_op jit(solution)/shard_map/ppermute | solution.py:15
  19.9 7.9 %collective-permute-start = (bf16[64,512]{1,0:T(8,128)(2,1)S(1)}, bf16[64,512]{1,0:T(8,128)(2,1)S(1)}, u32[]{:S(2)}, u32[]{:S(2)}) collective-permute-start(bf16[64,512]{1,0:T(8,128)(2,1)S(1)} %get-tuple-element.18), channel_id=1, source_target_pairs={{0,2},{2,4},{4,6},{6,8},{8,10},{10,12},{12,14},{14,16},{16,18},{18... | collective-permute-start | bytes 196616 | tf_op jit(solution)/shard_map/ppermute | solution.py:15
  28.5 1.0 copy-start.5
  29.5 0.9 copy-start.6
  29.5 0.9 copy-start.7
  30.9 1.1 copy-start
  32.0 1.5 copy-start.3
  36.2 196.6 %all-reduce.7.cloned.1.call-start = ((), (), s32[]{:S(2)}) async-start(), calls=%async_computation.1 | async-start | bytes 8388608 | tf_op jit(solution)/shard_map/psum | solution.py:9
  209.0 18.4 %collective-permute-start.7 = (bf16[64,512]{1,0:T(8,128)(2,1)S(1)}, bf16[64,512]{1,0:T(8,128)(2,1)}, u32[]{:S(2)}, u32[]{:S(2)}) collective-permute-start(bf16[64,512]{1,0:T(8,128)(2,1)S(1)} %get-tuple-element.15), channel_id=1, source_target_pairs={{0,1},{2,3},{4,5},{6,7},{8,9},{10,11},{12,13},{14,15},{16,17},{18,... | collective-permute-start | bytes 196616 | tf_op jit(solution)/shard_map/ppermute | solution.py:21
  211.0 16.4 %collective-permute-start.6 = (bf16[64,512]{1,0:T(8,128)(2,1)S(1)}, bf16[64,512]{1,0:T(8,128)(2,1)}, u32[]{:S(2)}, u32[]{:S(2)}) collective-permute-start(bf16[64,512]{1,0:T(8,128)(2,1)S(1)} %get-tuple-element.16), channel_id=1, source_target_pairs={{1,0},{3,2},{5,4},{7,6},{9,8},{11,10},{13,12},{15,14},{17,16},{19,... | collective-permute-start | bytes 196616 | tf_op jit(solution)/shard_map/ppermute | solution.py:21
  212.3 15.1 %collective-permute-start.5 = (bf16[64,512]{1,0:T(8,128)(2,1)S(1)}, bf16[64,512]{1,0:T(8,128)(2,1)}, u32[]{:S(2)}, u32[]{:S(2)}) collective-permute-start(bf16[64,512]{1,0:T(8,128)(2,1)S(1)} %get-tuple-element.17), channel_id=1, source_target_pairs={{0,2},{2,4},{4,6},{6,8},{8,10},{10,12},{12,14},{14,16},{16,18},{18... | collective-permute-start | bytes 196616 | tf_op jit(solution)/shard_map/ppermute | solution.py:15
  213.8 13.6 %collective-permute-start.4 = (bf16[64,512]{1,0:T(8,128)(2,1)S(1)}, bf16[64,512]{1,0:T(8,128)(2,1)}, u32[]{:S(2)}, u32[]{:S(2)}) collective-permute-start(bf16[64,512]{1,0:T(8,128)(2,1)S(1)} %get-tuple-element.14), channel_id=1, source_target_pairs={{0,30},{2,0},{4,2},{6,4},{8,6},{10,8},{12,10},{14,12},{16,14},{18,... | collective-permute-start | bytes 196616 | tf_op jit(solution)/shard_map/ppermute | solution.py:15
  220.5 6.9 %copy-start.9 = (s32[1,4,64]{2,1,0:T(4,128)S(1)}, s32[1,4,64]{2,1,0:T(4,128)}, u32[]{:S(2)}) copy-start(s32[1,4,64]{2,1,0:T(4,128)} %param.19) | copy-start | bytes 3076
  232.8 3.5 %copy-start.2 = (f32[512,512]{1,0:T(8,128)S(1)}, f32[512,512]{1,0:T(8,128)}, u32[]{:S(2)}) copy-start(f32[512,512]{1,0:T(8,128)} %get-tuple-element.13) | copy-start | bytes 3145732
Sparse Core Ops, SparseCore 0:
  36.3 166.5 all-reduce.4
  205.4 27.3 all-reduce.6
